TPU v7x, 16 devices: a whole 2x2x2 slice. The times are simulated.
16 devices in a mesh: sp: 16 (over z, y, x, core).
Axes of the slice: x: 2, y: 2, z: 2, core: 2. Of those that a mesh axis runs over, the one named last changes fastest.
Arguments:
- hidden: bfloat16 [32, 512, 1024], P(None, 'sp')
- norm_gain: float32 [1024], replicated
- w_q: bfloat16 [1024, 2048], replicated
- w_k: bfloat16 [1024, 1024], replicated
- w_v: bfloat16 [1024, 1024], replicated
- q_gain: float32 [128], replicated
- k_gain: float32 [128], replicated
- w_o: bfloat16 [2048, 1024], replicated
- d_out: bfloat16 [32, 512, 1024], P(None, 'sp')
Outputs:
- output 1: bfloat16 [32, 512, 1024], P(None, 'sp')
- output 2: bfloat16 [32, 512, 1024], P(None, 'sp')
- output 3: float32 [1024, 2048], replicated
- output 4: float32 [1024, 1024], replicated
- output 5: float32 [1024, 1024], replicated
- output 6: float32 [2048, 1024], replicated
- output 7: float32 [1024], replicated
- output 8: float32 [128], replicated
- output 9: float32 [128], replicated
All inputs are finite; a program needn't handle non-finite values.
Results may differ from a plain program's by a relative error of at most 0.0181044.
Values are sent between devices in bfloat16 or wider.
A program may use at most 1 GiB of HBM per device.

v0:
```python
import math
import jax
import jax.numpy as jnp
import numpy as np
from jax import lax
from jax.experimental import pallas as pl
from jax.experimental.pallas import tpu as pltpu
from jax.sharding import PartitionSpec as P

ROPE_BASE = 1000000.0
NORM_EPS = 1e-6
LOG2E = 1.4426950408889634
F32 = jnp.float32
BF16 = jnp.bfloat16
QBLK = 256
OUT_MASKS = (14, 12, 8, 6, 4, 10, 2, 15, 13, 9, 7, 5, 11, 3, 1)
AHEAD = 3
VMEM_LIMIT = 36640 * 1024
COLOURS = ((1, 2, 3), (2, 3, 1), (3, 1, 2))
PER_POINT = 4
MASKS = (8, 4, 2, 12, 10, 6, 14, 9, 5, 3, 13, 11, 7, 15, 1)


def dot(a, b, ca, cb):
    return lax.dot_general(a, b, (((ca,), (cb,)), ((), ())), preferred_element_type=F32)


def rope_tables(n_pos, head_dim):
    half_dim = head_dim // 2
    inv_freq = np.exp(np.arange(half_dim, dtype=np.float32) * np.float32(-2.0 * math.log(ROPE_BASE) / head_dim))
    angles = np.arange(n_pos, dtype=np.float32)[:, None] * inv_freq[None, :]
    cos, sin = np.cos(angles), np.sin(angles)
    return np.concatenate([cos, cos], axis=-1), np.concatenate([-sin, sin], axis=-1)


def norm_rope(raw, gain, cos, sin):
    inv = lax.rsqrt(jnp.mean(raw * raw, axis=-1, keepdims=True) + NORM_EPS)
    unit = raw * inv
    normed = unit * gain
    return normed * cos + pltpu.roll(normed, raw.shape[-1] // 2, 1) * sin, unit, inv


def norm_rope_back(d_rot, unit, inv, gain, cos, sin):
    d_normed = d_rot * cos - pltpu.roll(d_rot, unit.shape[-1] // 2, 1) * sin
    d_gain = jnp.sum(d_normed * unit, axis=0, keepdims=True)
    d_unit = d_normed * gain
    return inv * (d_unit - unit * jnp.mean(d_unit * unit, axis=-1, keepdims=True)), d_gain


def causal_mask_t(scores_t, first_q):
    n_q = scores_t.shape[1]
    key = lax.broadcasted_iota(jnp.int32, (n_q, n_q), 0)
    query = lax.broadcasted_iota(jnp.int32, (n_q, n_q), 1)
    diag = jnp.where(query >= key, scores_t[first_q:], -1e30)
    if first_q == 0:
        return diag
    return jnp.concatenate([scores_t[:first_q], diag], axis=0)


def block_kernel(n_groups, *refs):
    n_steps = n_groups + 4

    def body(step, carry):
        block_step(step, n_steps, n_groups, *refs)
        return carry
    lax.fori_loop(0, n_steps, body, 0)


def block_step(step, n_steps, n_groups, hid_ref, dyin_ref, gain_ref, wq_ref, wk_ref, wv_ref, wo_ref, qg_ref, kg_ref,
               cos_ref, sin_ref, y_ref, dx_ref, u, small_ref,
               xs, dys, hs, ht, wcats, wos, dqkv, oall, dqkv_early, o_early, y_acc, dn_acc, r0, r1, r2, r3, r4, sm, smr,
               in_send, in_recv, in_loc, d_send, d_recv, p_send, p_recv, g_send, g_recv, e_send, e_recv,
               s_send, s_recv, out_send, out_recv, out_loc, w_sem):
    n_dev, rows, n_loc, dim = hid_ref.shape
    n_pos = n_dev * n_loc
    head_dim = qg_ref.shape[-1]
    qw = wos.shape[1]
    group = qw // head_dim
    width = qw + 2 * head_dim
    half = u.shape[1] // 2
    lane = half // 2
    blk = lane // 3
    me = lax.axis_index('sp')
    bit = [(me // (1 << i)) % 2 for i in range(4)]
    partner = [me + (1 << i) * (1 - 2 * bit[i]) for i in range(4)]

    def remote(src, dst, send, recv, device):
        return pltpu.make_async_remote_copy(src_ref=src, dst_ref=dst, send_sem=send, recv_sem=recv,
                                            device_id=(device,), device_id_type=pl.DeviceIdType.MESH)

    def rows_of(g, start, size):
        return u.at[g, pl.ds(pl.multiple_of(start, 16), size)]

    own = [bit[0] * half + h * lane for h in range(2)]
    other = [(1 - bit[0]) * half + h * lane for h in range(2)]
    keep1, send1, keep2, send2, keep3, send3 = {}, {}, {}, {}, {}, {}
    for h in range(2):
        for c, (d1, d2, d3) in enumerate(COLOURS):
            base = own[h] + c * blk
            keep1[h, c] = base + bit[d1] * (blk // 2)
            send1[h, c] = base + (1 - bit[d1]) * (blk // 2)
            keep2[h, c] = keep1[h, c] + bit[d2] * (blk // 4)
            send2[h, c] = keep1[h, c] + (1 - bit[d2]) * (blk // 4)
            keep3[h, c] = keep2[h, c] + bit[d3] * (blk // 8)
            send3[h, c] = keep2[h, c] + (1 - bit[d3]) * (blk // 8)

    def core_scatter(g, h):
        return remote(rows_of(g, other[h], lane), r0.at[g % 2, h], d_send.at[h, g % 2], d_recv.at[h, g % 2], partner[0])

    def scatter(phase, c, g, h):
        start, size, buf = ((send1, blk // 2, r1), (send2, blk // 4, r2), (send3, blk // 8, r3))[phase]
        return remote(rows_of(g, start[h, c], size), buf.at[g % 2, h, c], p_send.at[phase, c, h, g % 2],
                      p_recv.at[phase, c, h, g % 2], partner[COLOURS[c][phase]])

    def gather(phase, c, g, h):
        start, size = ((keep3, blk // 8), (keep2, blk // 4), (keep1, blk // 2))[phase]
        part = rows_of(g, start[h, c], size)
        return remote(part, part if phase else r4.at[g % 2, h, c], g_send.at[phase, c, h, g % 2],
                      g_recv.at[phase, c, h, g % 2], partner[COLOURS[c][2 - phase]])

    def core_gather(g, h):
        part = rows_of(g, own[h], lane)
        return remote(part, part, e_send.at[h, g % 2], e_recv.at[h, g % 2], partner[0])

    def add_rows(g, start, size, buf):
        s = pl.ds(pl.multiple_of(start, 16), size)
        u[g, s] = u[g, s] + buf

    def stage(k, g, h):
        slot = g % 2
        if k == 1:
            core_scatter(g, h).wait()
            for c in range(3):
                add_rows(g, own[h] + c * blk, blk, r0[slot, h, c * blk:(c + 1) * blk])
                scatter(0, c, g, h).start()
        elif k in (2, 3, 4):
            keep, size, buf = ((keep1, blk // 2, r1), (keep2, blk // 4, r2), (keep3, blk // 8, r3))[k - 2]
            for c in range(3):
                scatter(k - 2, c, g, h).wait()
            for c in range(3):
                add_rows(g, keep[h, c], size, buf[slot, h, c])
                (scatter(k - 1, c, g, h) if k < 4 else gather(0, c, g, h)).start()
        elif k in (5, 6):
            for c in range(3):
                gather(k - 5, c, g, h).wait()
            for c in range(3):
                if k == 5:
                    u[g, pl.ds(pl.multiple_of(send3[h, c], 16), blk // 8)] = r4[slot, h, c]
                gather(k - 4, c, g, h).start()
        elif k == 7:
            for c in range(3):
                gather(2, c, g, h).wait()
            core_gather(g, h).start()
        else:
            core_gather(g, h).wait()

    sends = [(which, row, mask) for row in range(2) for which in (1, 0) for mask in OUT_MASKS]

    def handler(sub):
        h = sub % 2
        for k in range(8, 0, -1):
            if (2 * k - 2 + h - sub) % 4 == 0:
                g = step - 1 - (2 * k - 2 + h - sub) // 4

                @pl.when((g >= 0) & (g < n_groups))
                def _():
                    stage(k, g, h)
        for i in range(5):
            if (2 * i + 3) % 4 == sub:
                @pl.when(step == n_groups + (2 * i + 3) // 4)
                def _():
                    if i == 0:
                        small_copy(0).start()
                    else:
                        small_step(i - 1)
        for j in range(-(-len(sends) // PER_POINT)):
            if (j + 1) % 4 == sub:
                @pl.when(step == n_groups + (j + 1) // 4)
                def _():
                    for which, row, mask in sends[j * PER_POINT:(j + 1) * PER_POINT]:
                        to_peers(out_copy, which, row, (mask,))

    def small_copy(i):
        return remote(sm.at[i], smr.at[i], s_send.at[i], s_recv.at[i], partner[i])

    def small_step(i):
        small_copy(i).wait()
        sm[i + 1] = sm[i] + smr[i]
        if i < 3:
            small_copy(i + 1).start()
        else:
            small_ref[...] = sm[4]

    def in_copy(which, row, peer):
        src, dst = (hid_ref, xs) if which == 0 else (dyin_ref, dys)
        n = 2 * row + which
        return remote(src.at[peer, row], dst.at[row, me], in_send.at[n], in_recv.at[n], peer)

    def in_local(which, row):
        src, dst = (hid_ref, xs) if which == 0 else (dyin_ref, dys)
        return pltpu.make_async_copy(src.at[me, row], dst.at[row, me], in_loc.at[2 * row + which])

    def in_wait(which, row):
        dst = xs if which == 0 else dys
        n = 2 * row + which
        many = dst.at[row, pl.ds(0, n_dev - 1)]
        pltpu.make_async_copy(many, many, in_recv.at[n]).wait()
        in_local(which, row).wait()

    def in_wait_send(which, row):
        many = (xs if which == 0 else dys).at[row, pl.ds(0, n_dev - 1)]
        pltpu.make_async_copy(many, many, in_send.at[2 * row + which]).wait()

    def out_copy(which, row, peer):
        src, dst = (xs, y_ref) if which == 0 else (dys, dx_ref)
        n = 2 * row + which
        return remote(src.at[row, peer], dst.at[me, row], out_send.at[n], out_recv.at[n], peer)

    def out_local(which, row):
        src, dst = (xs, y_ref) if which == 0 else (dys, dx_ref)
        return pltpu.make_async_copy(src.at[row, me], dst.at[me, row], out_loc.at[2 * row + which])

    def to_peers(make, which, row, masks):
        for mask in masks:
            make(which, row, me + sum((mask & (1 << i)) * (1 - 2 * bit[i]) for i in range(4))).start()

    @pl.when(step == 0)
    def _():
        barrier = pltpu.get_barrier_semaphore()

        def greet(d, carry):
            pl.semaphore_signal(barrier, inc=1, device_id=(lax.rem(me + d, n_dev),), device_id_type=pl.DeviceIdType.MESH)
            return carry
        lax.fori_loop(1, n_dev, greet, 0)
        pl.semaphore_wait(barrier, n_dev - 1)
        for row in range(rows):
            for which in range(2):
                in_local(which, row).start()
                to_peers(in_copy, which, row, MASKS)
        y_acc[...] = jnp.zeros_like(y_acc)
        dn_acc[...] = jnp.zeros_like(dn_acc)
        sm[0] = jnp.zeros_like(sm[0])

    def tokens_of(row):
        return slice(row * n_pos, (row + 1) * n_pos)

    def row_compute(row, g, arriving, d_to, o_to):
        tok = tokens_of(row)
        wcat, wo = wcats.at[g % 2], wos.at[g % 2]
        cos, sin = cos_ref[...], sin_ref[...]
        scale = head_dim ** -0.5
        qkv = dot(hs[tok], wcat[...], 1, 0).astype(BF16)

        def grad_heads():
            return dot(dys[row].reshape(n_pos, dim), wo[...], 1, 1).astype(BF16)

        def probs_of(first, q_blk, cols):
            n_key = first + QBLK
            scores = causal_mask_t(dot(k_rot[:n_key], q_blk, 1, 1) * (scale * LOG2E), first)
            e = jnp.exp2(scores - jnp.max(scores, axis=0, keepdims=True))
            prob = e * (1.0 / jnp.sum(e, axis=0, keepdims=True))
            prob_bf = prob.astype(BF16)
            o_to[first:n_key, cols] = dot(prob_bf, v[:n_key], 0, 0).astype(BF16)
            return prob, prob_bf

        k_rot, k_unit, k_inv = norm_rope(qkv[:, qw:qw + head_dim].astype(F32), kg_ref[...], cos, sin)
        k_rot = k_rot.astype(BF16)
        v = qkv[:, qw + head_dim:]
        if arriving:
            early = []
            for j in range(group):
                cols = slice(j * head_dim, (j + 1) * head_dim)
                q_rot, q_unit, q_inv = norm_rope(qkv[:, cols].astype(F32), qg_ref[...], cos, sin)
                q_rot = q_rot.astype(BF16)
                early.append((q_rot, q_unit, q_inv, [probs_of(first, q_rot[first:first + QBLK], cols) for first in range(0, n_pos, QBLK)]))
            in_wait(1, row)
        d_o = grad_heads()
        dk_sum = [jnp.zeros((QBLK, head_dim), F32) for _ in range(n_pos // QBLK)]
        dv_sum = [jnp.zeros((QBLK, head_dim), F32) for _ in range(n_pos // QBLK)]
        for j in range(group):
            cols = slice(j * head_dim, (j + 1) * head_dim)
            if arriving:
                q_rot, q_unit, q_inv, probs = early[j]
            else:
                q_rot, q_unit, q_inv = norm_rope(qkv[:, cols].astype(F32), qg_ref[...], cos, sin)
                q_rot = q_rot.astype(BF16)
            dq_parts = []
            for first in range(0, n_pos, QBLK):
                n_key = first + QBLK
                q_blk = q_rot[first:n_key]
                do_blk = d_o[first:n_key, cols]
                prob, prob_bf = probs[first // QBLK] if arriving else probs_of(first, q_blk, cols)
                d_prob = dot(v[:n_key], do_blk, 1, 1)
                inner = jnp.sum(prob * d_prob, axis=0, keepdims=True)
                d_scores = (prob * (d_prob - inner)).astype(BF16)
                dv_blk = dot(prob_bf, do_blk, 1, 0)
                dk_blk = dot(d_scores, q_blk, 1, 0)
                for i in range(n_key // QBLK):
                    dv_sum[i] += dv_blk[i * QBLK:(i + 1) * QBLK]
                    dk_sum[i] += dk_blk[i * QBLK:(i + 1) * QBLK]
                dq_parts.append(dot(d_scores, k_rot[:n_key], 0, 0))
            dq = (jnp.concatenate(dq_parts, axis=0) * scale).astype(BF16).astype(F32)
            dq_raw, d_gain = norm_rope_back(dq, q_unit, q_inv, qg_ref[...], cos, sin)
            d_to[:, cols] = dq_raw.astype(BF16)
            sm[0, 1:2, :head_dim] += d_gain
        dk = (jnp.concatenate(dk_sum, axis=0) * scale).astype(BF16).astype(F32)
        dk_raw, d_gain = norm_rope_back(dk, k_unit, k_inv, kg_ref[...], cos, sin)
        d_to[:, qw:qw + head_dim] = dk_raw.astype(BF16)
        sm[0, 1:2, head_dim:2 * head_dim] += d_gain
        d_to[:, qw + head_dim:] = jnp.concatenate(dv_sum, axis=0).astype(BF16)

    def input_norm(row):
        x = xs[row].reshape(n_pos, dim).astype(F32)
        inv = lax.rsqrt(jnp.mean(x * x, axis=-1, keepdims=True) + NORM_EPS)
        h = (x * inv * gain_ref[...]).astype(BF16)
        hs[tokens_of(row)] = h
        ht[:, tokens_of(row)] = h.T

    def finish_row(row):
        tok = tokens_of(row)
        x = xs[row].reshape(n_pos, dim).astype(F32)
        inv = lax.rsqrt(jnp.mean(x * x, axis=-1, keepdims=True) + NORM_EPS)
        unit = x * inv
        d_normed = dn_acc[tok]
        sm[0, 0:1] += jnp.sum(d_normed * unit, axis=0, keepdims=True)
        d_unit = d_normed * gain_ref[...]
        d_x = inv * (d_unit - unit * jnp.mean(d_unit * unit, axis=-1, keepdims=True))
        d_y = dys[row].reshape(n_pos, dim).astype(F32)
        dys[row] = (d_y + d_x).astype(BF16).reshape(n_dev, n_loc, dim)
        xs[row] = (x + y_acc[tok]).astype(BF16).reshape(n_dev, n_loc, dim)

    computing = step < n_groups

    def weight_copies(g):
        slot = g % 2
        col = lambda n: pl.ds(pl.multiple_of(g * n, 128), n)
        pieces = ((wq_ref.at[:, col(qw)], wcats.at[slot, :, :qw]),
                  (wk_ref.at[:, col(head_dim)], wcats.at[slot, :, qw:qw + head_dim]),
                  (wv_ref.at[:, col(head_dim)], wcats.at[slot, :, qw + head_dim:]),
                  (wo_ref.at[col(qw)], wos.at[slot]))
        return [pltpu.make_async_copy(a, b, w_sem.at[slot, i]) for i, (a, b) in enumerate(pieces)]

    def weights(g, n):
        for copy in weight_copies(g):
            copy.wait()

        @pl.when(g + 1 < n)
        def _():
            for copy in weight_copies(g + 1):
                copy.start()

    @pl.when(step == 0)
    def _():
        for copy in weight_copies(0):
            copy.start()
        in_wait(0, 0)
        input_norm(0)
        in_wait(1, 0)

        def first_row(g, carry):
            weights(g, AHEAD)
            row_compute(0, g, False, dqkv_early.at[g], o_early.at[g])
            return carry
        lax.fori_loop(0, AHEAD, first_row, 0)
        for copy in weight_copies(0):
            copy.start()
        in_wait(0, 1)
        input_norm(1)

    @pl.when(computing)
    def _():
        weights(step, n_groups)

    for row in range(rows):
        handler(row)

        if row == 0:
            @pl.when(step < AHEAD)
            def _():
                dqkv[:n_pos] = dqkv_early[step]
                oall[:n_pos] = o_early[step]

        def into(row, arriving):
            row_compute(row, step, arriving, dqkv.at[tokens_of(row)], oall.at[tokens_of(row)])

        if row == 1:
            @pl.when(step == 0)
            def _():
                into(row, True)

        @pl.when(computing & (step >= (AHEAD if row == 0 else 1)))
        def _():
            into(row, False)

        @pl.when(step == n_groups)
        def _():
            for which in range(2):
                in_wait_send(which, row)
            finish_row(row)
            for which in range(2):
                out_local(which, row).start()

    handler(2)

    @pl.when(computing)
    def _():
        u[step, :dim] = dot(ht[...], dqkv[...], 1, 0)
        d_wo = dot(oall[...], dys[...].reshape(rows * n_pos, dim), 0, 0)
        u[step, dim:dim + qw] = d_wo[:, :width]
        u[step, dim + qw:] = d_wo[:, width:]
        for h in range(2):
            core_scatter(step, h).start()

    handler(3)

    @pl.when(computing)
    def _():
        y_acc[...] += dot(oall[...], wos[step % 2], 1, 0)
        dn_acc[...] += dot(dqkv[...], wcats[step % 2], 1, 1)

    @pl.when(step == n_steps - 1)
    def _():
        for row in range(rows):
            for which in range(2):
                n = 2 * row + which
                many = (xs if which == 0 else dys).at[row, pl.ds(0, n_dev - 1)]
                landed = (y_ref if which == 0 else dx_ref).at[pl.ds(0, n_dev - 1), row]
                pltpu.make_async_copy(many, many, out_send.at[n]).wait()
                pltpu.make_async_copy(landed, landed, out_recv.at[n]).wait()
                out_local(which, row).wait()


def place_kernel(y_in, dx_in, u, small, y_ref, dx_ref, dwq_ref, dwk_ref, dwv_ref, dwo_ref, dg_ref, dqg_ref, dkg_ref,
                 out_sem, w_sem, s_sem):
    dim, head_dim = dg_ref.shape[1], dqg_ref.shape[1]
    n_groups, _, width = u.shape
    qw = dwq_ref.shape[1] // n_groups
    stores = []
    for g in range(n_groups):
        col = lambda n: slice(g * n, (g + 1) * n)
        pieces = ((u.at[g, :dim, :qw], dwq_ref.at[:, col(qw)]),
                  (u.at[g, :dim, qw:qw + head_dim], dwk_ref.at[:, col(head_dim)]),
                  (u.at[g, :dim, qw + head_dim:], dwv_ref.at[:, col(head_dim)]),
                  (u.at[g, dim:dim + qw], dwo_ref.at[col(qw), :width]),
                  (u.at[g, dim + qw:], dwo_ref.at[col(qw), width:]))
        stores += [pltpu.make_async_copy(src, dst, w_sem.at[g, i]) for i, (src, dst) in enumerate(pieces)]
    stores += [pltpu.make_async_copy(src, dst, s_sem.at[i]) for i, (src, dst) in enumerate((
        (small.at[0:1], dg_ref), (small.at[1:2, :head_dim], dqg_ref), (small.at[1:2, head_dim:2 * head_dim], dkg_ref)))]
    stores += [pltpu.make_async_copy(src, dst, out_sem.at[i]) for i, (src, dst) in enumerate(((y_in, y_ref), (dx_in, dx_ref)))]
    for copy in stores:
        copy.start()
    for copy in stores:
        copy.wait()


def solution(mesh):
    n_dev = mesh.shape['sp']
    seq_spec = P(None, 'sp', None)
    replicated = P()

    def local_step(hidden, norm_gain, w_q, w_k, w_v, q_gain, k_gain, w_o, d_out):
        n_batch, n_loc, dim = hidden.shape
        head_dim = q_gain.shape[0]
        kv_heads = w_k.shape[1] // head_dim
        qw = w_q.shape[1] // kv_heads
        width = qw + 2 * head_dim
        rows = n_batch // n_dev
        n_pos = n_loc * n_dev
        tokens = rows * n_pos
        cos, sin = rope_tables(n_pos, head_dim)
        slice_rows = dim + 2 * qw
        lane = slice_rows // 4
        blk = lane // 3
        anywhere = pl.BlockSpec(memory_space=pl.ANY)
        in_vmem = pl.BlockSpec(memory_space=pltpu.VMEM)
        act = (n_dev, rows, n_loc, dim)
        dma = pltpu.SemaphoreType.DMA
        y, d_hidden, slices, small = pl.pallas_call(
            lambda *refs: block_kernel(kv_heads, *refs),
            in_specs=[anywhere, anywhere, in_vmem, anywhere, anywhere, anywhere, anywhere] + [in_vmem] * 4,
            out_specs=[in_vmem] * 4,
            out_shape=[
                pltpu.VMEM(act, BF16), pltpu.VMEM(act, BF16),
                pltpu.VMEM((kv_heads, slice_rows, width), F32), pltpu.VMEM((8, dim), F32)],
            scratch_shapes=[
                pltpu.VMEM((rows, n_dev, n_loc, dim), BF16), pltpu.VMEM((rows, n_dev, n_loc, dim), BF16),
                pltpu.VMEM((tokens, dim), BF16), pltpu.VMEM((dim, tokens), BF16),
                pltpu.VMEM((2, dim, width), BF16), pltpu.VMEM((2, qw, dim), BF16),
                pltpu.VMEM((tokens, width), BF16), pltpu.VMEM((tokens, qw), BF16),
                pltpu.VMEM((AHEAD, n_pos, width), BF16), pltpu.VMEM((AHEAD, n_pos, qw), BF16),
                pltpu.VMEM((tokens, dim), F32), pltpu.VMEM((tokens, dim), F32),
                pltpu.VMEM((2, 2, lane, width), F32), pltpu.VMEM((2, 2, 3, blk // 2, width), F32),
                pltpu.VMEM((2, 2, 3, blk // 4, width), F32), pltpu.VMEM((2, 2, 3, blk // 8, width), F32),
                pltpu.VMEM((2, 2, 3, blk // 8, width), F32),
                pltpu.VMEM((5, 8, dim), F32), pltpu.VMEM((4, 8, dim), F32),
                dma((4,)), dma((4,)), dma((4,)), dma((2, 2)), dma((2, 2)), dma((3, 3, 2, 2)), dma((3, 3, 2, 2)),
                dma((3, 3, 2, 2)), dma((3, 3, 2, 2)), dma((2, 2)), dma((2, 2)), dma((4,)), dma((4,)),
                dma((4,)), dma((4,)), dma((4,)), dma((2, 4))],
            compiler_params=pltpu.CompilerParams(
                vmem_limit_bytes=VMEM_LIMIT, collective_id=0, has_side_effects=True),
            cost_estimate=pl.CostEstimate(flops=52 * 10**9, bytes_accessed=50 * 10**6, transcendentals=0),
            name='attn_block',
        )(hidden.reshape(act), d_out.reshape(act), norm_gain[None], w_q, w_k, w_v, w_o, q_gain[None], k_gain[None],
          jnp.asarray(cos), jnp.asarray(sin))
        y, d_hidden, d_wq, d_wk, d_wv, d_wo, d_ng, d_qg, d_kg = pl.pallas_call(
            place_kernel,
            in_specs=[in_vmem] * 4,
            out_specs=[anywhere] * 9,
            out_shape=[
                jax.ShapeDtypeStruct(act, BF16), jax.ShapeDtypeStruct(act, BF16),
                jax.ShapeDtypeStruct(w_q.shape, F32), jax.ShapeDtypeStruct(w_k.shape, F32),
                jax.ShapeDtypeStruct(w_v.shape, F32), jax.ShapeDtypeStruct(w_o.shape, F32),
                jax.ShapeDtypeStruct((1, dim), F32), jax.ShapeDtypeStruct((1, head_dim), F32),
                jax.ShapeDtypeStruct((1, head_dim), F32)],
            scratch_shapes=[dma((2,)), dma((kv_heads, 5)), dma((3,))],
            compiler_params=pltpu.CompilerParams(vmem_limit_bytes=4 * 1024 * 1024),
            cost_estimate=pl.CostEstimate(flops=10**9, bytes_accessed=60 * 10**6, transcendentals=0),
            name='pack_out',
        )(*[pltpu.with_memory_space_constraint(a, pltpu.VMEM) for a in (y, d_hidden, slices, small)])
        return (y.reshape(hidden.shape), d_hidden.reshape(hidden.shape), d_wq, d_wk, d_wv, d_wo, d_ng[0], d_qg[0], d_kg[0])

    return jax.shard_map(local_step, mesh=mesh, in_specs=(seq_spec, replicated, replicated, replicated, replicated, replicated, replicated, replicated, seq_spec), out_specs=(seq_spec, seq_spec, replicated, replicated, replicated, replicated, replicated, replicated, replicated), check_vma=False)
```

profile of v0, /device:TPU:0, one launch (start us, length us, event | category | flops | bytes accessed | tf_op | source)
XLA Modules:
  0.0 278.6 jit_solution(7522934947452804386)
XLA Ops:
  0.6 267.9 %attn_block.1 = (bf16[16,2,32,1024]{3,2,1,0:T(8,128)(2,1)S(1)}, bf16[16,2,32,1024]{3,2,1,0:T(8,128)(2,1)S(1)}, f32[8,1536,512]{2,1,0:T(8,128)S(1)}, f32[8,1024]{1,0:T(8,128)S(1)}) custom-call(bf16[16,2,32,1024]{3,2,1,0:T(8,128)(2,1)} %bitcast.10, bf16[16,2,32,1024]{3,2,1,0:T(8,128)(2,1)} %bitcast.11, f32[1,1024]{1,0:T(1,128)} %bitcast.14, ...), custom_call_target="tpu_custom_call" | custom-call | flops 51999997952 | bytes 50000000 | tf_op jit(solution)/shard_map/attn_block/pallas_call | solution.py:478
  268.6 10.0 %pack_out.1 = (bf16[16,2,32,1024]{3,2,1,0:T(8,128)(2,1)}, bf16[16,2,32,1024]{3,2,1,0:T(8,128)(2,1)}, f32[1024,2048]{1,0:T(8,128)}, f32[1024,1024]{1,0:T(8,128)},...) custom-call(bf16[16,2,32,1024]{3,2,1,0:T(8,128)(2,1)S(1)} %get-tuple, ...), custom_call_target="tpu_custom_call" | custom-call | flops 1000000000 | bytes 60000000 | tf_op jit(solution)/shard_map/pack_out/pallas_call | solution.py:505
where the time goes:
time: 279 us
  Pallas kernels  278 us (100%)
    pallas_call x1, Pallas kernels, local_step(): pl.pallas_call(lambda *refs: block_kernel(kv_heads, *refs), in_specs=[any...  268 us
    pallas_call x1, Pallas kernels, local_step(): pl.pallas_call(place_kernel, in_specs=[in_vmem] * 4, out_specs=[anywhere]...  10 us

commit v1 on v0

--- a/solution.py
+++ b/solution.py
@@ -51,7 +51,7 @@
     n_q = scores_t.shape[1]
     key = lax.broadcasted_iota(jnp.int32, (n_q, n_q), 0)
     query = lax.broadcasted_iota(jnp.int32, (n_q, n_q), 1)
-    diag = jnp.where(query >= key, scores_t[first_q:], -1e30)
+    diag = jnp.where(query >= key, scores_t[first_q:], -1e30 * LOG2E)
     if first_q == 0:
         return diag
     return jnp.concatenate([scores_t[:first_q], diag], axis=0)
@@ -292,18 +292,18 @@
                 prob, prob_bf = probs[first // QBLK] if arriving else probs_of(first, q_blk, cols)
                 d_prob = dot(v[:n_key], do_blk, 1, 1)
                 inner = jnp.sum(prob * d_prob, axis=0, keepdims=True)
-                d_scores = (prob * (d_prob - inner)).astype(BF16)
+                d_scores = (prob * (d_prob - inner) * scale).astype(BF16)
                 dv_blk = dot(prob_bf, do_blk, 1, 0)
                 dk_blk = dot(d_scores, q_blk, 1, 0)
                 for i in range(n_key // QBLK):
                     dv_sum[i] += dv_blk[i * QBLK:(i + 1) * QBLK]
                     dk_sum[i] += dk_blk[i * QBLK:(i + 1) * QBLK]
                 dq_parts.append(dot(d_scores, k_rot[:n_key], 0, 0))
-            dq = (jnp.concatenate(dq_parts, axis=0) * scale).astype(BF16).astype(F32)
+            dq = jnp.concatenate(dq_parts, axis=0).astype(BF16).astype(F32)
             dq_raw, d_gain = norm_rope_back(dq, q_unit, q_inv, qg_ref[...], cos, sin)
             d_to[:, cols] = dq_raw.astype(BF16)
             sm[0, 1:2, :head_dim] += d_gain
-        dk = (jnp.concatenate(dk_sum, axis=0) * scale).astype(BF16).astype(F32)
+        dk = jnp.concatenate(dk_sum, axis=0).astype(BF16).astype(F32)
         dk_raw, d_gain = norm_rope_back(dk, k_unit, k_inv, kg_ref[...], cos, sin)
         d_to[:, qw:qw + head_dim] = dk_raw.astype(BF16)
         sm[0, 1:2, head_dim:2 * head_dim] += d_gain

time: 279 us -> 279 us (level)
  no operation moved by 1% of the time
where the time goes in v1:
time: 279 us; the launch traced here: 278 us
  Pallas kernels  278 us (100%)
    pallas_call x1, Pallas kernels, local_step(): pl.pallas_call(lambda *refs: block_kernel(kv_heads, *refs), in_specs=[any...  268 us
    pallas_call x1, Pallas kernels, local_step(): pl.pallas_call(place_kernel, in_specs=[in_vmem] * 4, out_specs=[anywhere]...  10 us

profile of v1, /device:TPU:0, one launch (start us, length us, event | category | flops | bytes accessed | tf_op | source)
XLA Modules:
  0.0 278.5 jit_solution(1084879722909209234)
XLA Ops:
  0.6 267.8 %attn_block.1 = (bf16[16,2,32,1024]{3,2,1,0:T(8,128)(2,1)S(1)}, bf16[16,2,32,1024]{3,2,1,0:T(8,128)(2,1)S(1)}, f32[8,1536,512]{2,1,0:T(8,128)S(1)}, f32[8,1024]{1,0:T(8,128)S(1)}) custom-call(bf16[16,2,32,1024]{3,2,1,0:T(8,128)(2,1)} %bitcast.10, bf16[16,2,32,1024]{3,2,1,0:T(8,128)(2,1)} %bitcast.11, f32[1,1024]{1,0:T(1,128)} %bitcast.14, ...), custom_call_target="tpu_custom_call" | custom-call | flops 51999997952 | bytes 50000000 | tf_op jit(solution)/shard_map/attn_block/pallas_call | solution.py:478
  268.4 10.0 %pack_out.1 = (bf16[16,2,32,1024]{3,2,1,0:T(8,128)(2,1)}, bf16[16,2,32,1024]{3,2,1,0:T(8,128)(2,1)}, f32[1024,2048]{1,0:T(8,128)}, f32[1024,1024]{1,0:T(8,128)},...) custom-call(bf16[16,2,32,1024]{3,2,1,0:T(8,128)(2,1)S(1)} %get-tuple, ...), custom_call_target="tpu_custom_call" | custom-call | flops 1000000000 | bytes 60000000 | tf_op jit(solution)/shard_map/pack_out/pallas_call | solution.py:505
